TPU v7x, 32 devices: a whole 2x2x4 slice. The times are simulated.
32 devices in a mesh: pts: 8 (over y, x, core), wid: 4 (over z).
Axes of the slice: x: 2, y: 2, z: 4, core: 2. Of those that a mesh axis runs over, the one named last changes fastest.
Arguments:
- vertex_features: bfloat16 [90112, 512], P('pts'), may hold values from -40 to 40, as said below
- entry_matrix: bfloat16 [512, 512], P(None, 'wid'), may hold values from -2 to 2, as said below
- partition_matrix: bfloat16 [64, 32], replicated, may hold values from -3 to 3, as said below
- sharpness_matrix: float32 [64], replicated, may hold values from -3 to 3, as said below
- summary_qkv_matrix: float32 [3, 64, 64], replicated, may hold values from -3 to 3
- exit_matrix: bfloat16 [512, 512], P('wid'), may hold values from -0.5 to 0.5
- widening_matrix: bfloat16 [512, 512], P('wid'), may hold values from -0.25 to 0.25
- narrowing_matrix: bfloat16 [512, 512], P('wid'), may hold values from -0.25 to 0.25
Outputs:
- result: bfloat16 [90112, 512], P(('pts', 'wid'))
Inputs may be any that keep to these rules, and one draw needn't show every extreme that they name: `vertex_features`: features of the points, of order one to ten. `entry_matrix`: weights of the point projection. `partition_matrix`: slice logit weights. `sharpness_matrix`: temperature weights.
All inputs are finite; a program needn't handle non-finite values.
Results may differ from a plain program's by a relative error of at most 0.013.
Values may be sent and summed in bfloat16 or wider, within the bound.
A program may use at most 128 MiB of HBM per device.

v0:
```python
import jax
import jax.numpy as jnp
from jax import lax
from jax.sharding import PartitionSpec as P


def layer_norm(values):
    centred = values - jnp.mean(values, axis=-1, keepdims=True)
    variance = jnp.mean(centred * centred, axis=-1, keepdims=True)
    return centred * lax.rsqrt(variance + 1e-05)


def project_tokens(token_rows, summary_qkv_matrix):
    highest = lax.Precision.HIGHEST
    queries = jnp.einsum("hgd,de->hge", token_rows, summary_qkv_matrix[0], precision=highest)
    keys_all = jnp.einsum("hgd,de->hge", token_rows, summary_qkv_matrix[1], precision=highest)
    value_rows_total = jnp.einsum(
        "hgd,de->hge", token_rows, summary_qkv_matrix[2], precision=highest
    )
    return (queries, keys_all, value_rows_total)


def local(
    vertex_features,
    entry_matrix,
    partition_matrix,
    sharpness_matrix,
    summary_qkv_matrix,
    exit_matrix,
    widening_matrix,
    narrowing_matrix,
):
    head_size = summary_qkv_matrix.shape[1]
    point_rows = vertex_features.shape[0]
    wid_count = lax.axis_size("wid")
    row_block = point_rows // wid_count
    features = vertex_features.astype(jnp.float32)
    normed = layer_norm(features).astype(jnp.bfloat16)
    feats = jnp.dot(normed, entry_matrix, preferred_element_type=jnp.float32).astype(jnp.bfloat16)
    local_heads = feats.shape[1] // head_size
    attention_cluster = feats.reshape(point_rows, local_heads, head_size)
    partition_sharpness = 0.5 + jax.nn.softplus(
        jnp.einsum(
            "kgv,v->kg", attention_cluster, sharpness_matrix, preferred_element_type=jnp.float32
        )
    )
    partition_scores = jnp.einsum(
        "nhd,dg->nhg", attention_cluster, partition_matrix, preferred_element_type=jnp.float32
    )
    partition_mapping = jax.nn.softmax(
        partition_scores / partition_sharpness[:, :, None], axis=-1
    ).astype(jnp.bfloat16)
    numerator = jnp.einsum(
        "nhg,nhd->hgd", partition_mapping, attention_cluster, preferred_element_type=jnp.float32
    )
    mass = jnp.sum(partition_mapping, axis=0, dtype=jnp.float32)
    numerator, mass = lax.psum((numerator, mass), "pts")
    token_rows = numerator / (mass[:, :, None] + 1e-05)
    queries, keys_all, value_rows_total = project_tokens(token_rows, summary_qkv_matrix)
    highest = lax.Precision.HIGHEST
    scores = jnp.einsum("hge,hke->hgk", queries, keys_all, precision=highest) / jnp.sqrt(
        jnp.float32(head_size)
    )
    attend = jax.nn.softmax(scores, axis=-1)
    out_tok = jnp.einsum("hgk,hke->hge", attend, value_rows_total, precision=highest).astype(
        jnp.bfloat16
    )
    deslice = jnp.einsum(
        "nhg,hgd->nhd", partition_mapping, out_tok, preferred_element_type=jnp.float32
    ).astype(jnp.bfloat16)
    deslice = deslice.reshape(point_rows, local_heads * head_size)
    mixed_rows = lax.all_to_all(deslice, "wid", split_axis=0, concat_axis=1, tiled=True)
    out_full, up_full, down_full = (
        lax.all_gather(exit_matrix, "wid", axis=0, tiled=True),
        lax.all_gather(widening_matrix, "wid", axis=0, tiled=True),
        lax.all_gather(narrowing_matrix, "wid", axis=0, tiled=True),
    )
    attn_rows = jnp.dot(mixed_rows, out_full, preferred_element_type=jnp.float32)
    own_rows = lax.dynamic_slice_in_dim(features, lax.axis_index("wid") * row_block, row_block, 0)
    midway = own_rows + attn_rows
    normed2 = layer_norm(midway).astype(jnp.bfloat16)
    hidden = jax.nn.gelu(jnp.dot(normed2, up_full, preferred_element_type=jnp.float32)).astype(
        jnp.bfloat16
    )
    return (midway + jnp.dot(hidden, down_full, preferred_element_type=jnp.float32)).astype(
        jnp.bfloat16
    )


def solution(mesh):
    placed = (
        P("pts", None),
        P(None, "wid"),
        P(),
        P(),
        P(),
        P("wid", None),
        P("wid", None),
        P("wid", None),
    )
    return jax.shard_map(
        local, mesh=mesh, in_specs=placed, out_specs=P(("pts", "wid"), None), check_vma=False
    )
```

profile of v0, /device:TPU:0, one launch (start us, length us, event | category | flops | bytes accessed | tf_op | source)
XLA Modules:
  0.0 224.7 jit_solution(1888954604760041601)
XLA Ops:
  0.0 0.0 copy-start
  0.0 14.9 %copy.12 = bf16[11264,512]{0,1:T(8,128)(2,1)} copy(bf16[11264,512]{1,0:T(8,128)(2,1)} %param.8) | data formatting | bytes 23068672 | tf_op args[0]
  14.9 7.2 %convert_reduce_fusion = f32[11264]{0:T(1024)S(1)} fusion(bf16[11264,512]{0,1:T(8,128)(2,1)} %copy.12), kind=kLoop, calls=%fused_computation.3 | loop fusion | flops 11523072 | bytes 11579392 | tf_op jit(solution)/shard_map/reduce_sum | solution.py:8
  22.0 7.4 %multiply_reduce_fusion = f32[11264]{0:T(1024)S(1)} fusion(bf16[11264,512]{0,1:T(8,128)(2,1)} %copy.12, f32[11264]{0:T(1024)S(1)} %broadcast_multiply_fusion), kind=kLoop, calls=%fused_computation.2 | loop fusion | flops 23057408 | bytes 11624448 | tf_op jit(solution)/shard_map/reduce_sum | solution.py:9
  29.5 0.0 copy-done
  29.5 0.0 copy-start.6
  29.5 8.1 %convolution_convert_fusion.1 = bf16[11264,128]{0,1:T(8,128)(2,1)S(1)} fusion(bf16[512,128]{1,0:T(8,128)(2,1)S(1)} %copy-done, bf16[11264,512]{0,1:T(8,128)(2,1)} %copy.12, f32[11264]{0:T(1024)S(1)} %add_rsqrt_fusion, f32[11264]{0:T(1024)S(1)} %broadcast_multiply_fusion), kind=kOutput, calls=%fused_computation.5 | convolution fusion | flops 1500905472 | bytes 14639104 | tf_op jit(solution)/shard_map/dot_general | solution.py:39
  37.6 0.0 copy-start.3
  37.6 0.0 copy-done.6
  37.6 5.4 %fusion.48 = f32[1,11264,2]{0,1,2:T(8,128)} fusion(bf16[11264,2,64]{0,2,1:T(8,128)(2,1)S(1)} %bitcast.68, f32[64]{0:T(128)S(1)} %copy-done.6), kind=kOutput, calls=%fused_computation.70 | convolution fusion | flops 2883584 | bytes 2973952 | tf_op jit(solution)/shard_map/kgv,v->kg/dot_general | solution.py:43
  43.0 0.0 copy-start.8
  43.0 6.6 %copy.16 = f32[1,11264,2]{1,2,0:T(2,128)S(1)} copy(f32[1,11264,2]{0,1,2:T(8,128)} %fusion.48) | data formatting | bytes 180224 | tf_op jit(solution)/shard_map/kgv,v->kg/dot_general | solution.py:43
  49.6 0.2 fusion.17
  49.8 0.0 copy-done.3
  49.8 0.0 copy-done.8
  49.8 2.9 %fusion.43 = (f32[11264,2]{0,1:T(2,128)S(1)}, f32[11264,2,32]{0,2,1:T(8,128)}) fusion(bf16[11264,2,64]{0,2,1:T(8,128)(2,1)S(1)} %bitcast.69, f32[11264,2]{0,1:T(2,128)S(1)} %fusion.17, bf16[64,32]{0,1:T(8,128)(2,1)S(1)} %copy-done.8), kind=kOutput, calls=%fused_computation.67 | convolution fusion | flops 94437408 | bytes 5951488 | tf_op jit(solution)/shard_map/sub | solution.py:50
  52.7 0.0 copy-start.7
  52.7 2.3 %convert_reduce_fusion.1 = (f32[2,32]{1,0:T(2,128)S(1)}, bf16[11264,2,32]{0,2,1:T(8,128)(2,1)S(1)}) fusion(f32[11264,2,32]{0,2,1:T(8,128)} %get-tuple-element.10, f32[11264,2]{0,1:T(2,128)S(1)} %get-tuple-element.9), kind=kLoop, calls=%fused_computation.28 | loop fusion | flops 2883520 | bytes 4415744 | tf_op jit(solution)/shard_map/reduce_sum | solution.py:56
  55.1 2.7 %fusion.51 = f32[2,32,64]{2,1,0:T(8,128)S(1)} fusion(bf16[11264,2,32]{0,2,1:T(8,128)(2,1)S(1)} %get-tuple-element.8, bf16[11264,2,64]{0,2,1:T(8,128)(2,1)} %bitcast.70), kind=kOutput, calls=%fused_computation.72 | convolution fusion | flops 92274688 | bytes 4341760 | tf_op jit(solution)/shard_map/nhg,nhd->hgd/dot_general | solution.py:53
  57.7 25.9 %all-reduce = (f32[2,32,64]{2,1,0:T(8,128)S(1)}, f32[2,32]{1,0:T(2,128)S(1)}) all-reduce(f32[2,32,64]{2,1,0:T(8,128)S(1)} %fusion.51, f32[2,32]{1,0:T(2,128)S(1)} %get-tuple-element.7), channel_id=1, replica_groups=mesh['pts'=8,'wid'=4] {'pts'}, use_global_device_ids=true, to_apply=%region_4.5 | all-reduce | flops 4160 | bytes 33280 | tf_op jit(solution)/shard_map/psum | solution.py:57
  83.6 0.0 copy-done.7
  83.6 0.2 fusion.24
  83.8 0.2 fusion.26
  84.1 0.2 fusion.22
  84.3 0.2 fusion.44
  84.6 0.3 convolution_convert_fusion.2
  84.8 2.5 %fusion.2 = bf16[11264,2,64]{0,2,1:T(8,128)(2,1)} fusion(bf16[2,32,64]{2,1,0:T(8,128)(2,1)S(1)} %convolution_convert_fusion.2, bf16[11264,2,32]{0,2,1:T(8,128)(2,1)S(1)} %get-tuple-element.8), kind=kOutput, calls=%fused_computation.7 | convolution fusion | flops 93716480 | bytes 4333568 | tf_op jit(solution)/shard_map/nhg,hgd->nhd/dot_general | solution.py:68
  87.3 5.3 %all_to_all.14 = bf16[4,2816,128]{1,0,2:T(4,128)(2,1)S(1)} reshape(bf16[11264,2,64]{0,2,1:T(8,128)(2,1)} %fusion.2) | data formatting | bytes 5767168 | tf_op jit(solution)/shard_map/all_to_all | solution.py:72
  92.6 1.9 copy.13
  94.5 4.9 %all-to-all-start = ((bf16[4,2816,128]{1,2,0:T(8,128)(2,1)}), bf16[4,2816,128]{1,2,0:T(8,128)(2,1)S(1)}, u32[]{:S(2)}, u32[]{:S(2)}) async-start(bf16[4,2816,128]{1,2,0:T(8,128)(2,1)} %copy.13), calls=%async_computation | async-start | bytes 5767168 | tf_op jit(solution)/shard_map/all_to_all | solution.py:72
  99.4 0.0 copy-start.5
  99.4 13.0 %convert_element_type.33 = f32[11264,512]{0,1:T(8,128)} convert(bf16[11264,512]{0,1:T(8,128)(2,1)} %copy.12) | non-fusion elementwise | flops 5767168 | bytes 34603008 | tf_op jit(solution)/shard_map/convert_element_type | solution.py:37
  112.3 0.0 copy-done.5
  112.3 60.0 %all_gather.9 = bf16[512,512]{1,0:T(8,128)(2,1)S(1)} all-gather(bf16[128,512]{1,0:T(8,128)(2,1)S(1)} %copy-done.5), channel_id=1, replica_groups=mesh['pts'=8,'wid'=4] {'wid'}, dimensions={0}, use_global_device_ids=true | all-gather | bytes 655360 | tf_op jit(solution)/shard_map/all_gather | solution.py:74
  172.3 17.7 %all_gather.10 = bf16[512,512]{1,0:T(8,128)(2,1)} all-gather(bf16[128,512]{1,0:T(8,128)(2,1)} %param.14), channel_id=1, replica_groups=mesh['pts'=8,'wid'=4] {'wid'}, dimensions={0}, use_global_device_ids=true | all-gather | bytes 655360 | tf_op jit(solution)/shard_map/all_gather | solution.py:75
  190.1 16.3 %all_gather.11 = bf16[512,512]{1,0:T(8,128)(2,1)} all-gather(bf16[128,512]{1,0:T(8,128)(2,1)} %param.15), channel_id=1, replica_groups=mesh['pts'=8,'wid'=4] {'wid'}, dimensions={0}, use_global_device_ids=true | all-gather | bytes 655360 | tf_op jit(solution)/shard_map/all_gather | solution.py:76
  206.3 0.0 all-to-all-done
  206.3 4.4 %fusion.45 = (f32[2816]{0:T(1024)S(1)}, f32[2816,512]{0,1:T(8,128)S(1)}) fusion(bf16[2816,512]{0,1:T(8,128)(2,1)S(1)} %bitcast.67, bf16[512,512]{1,0:T(8,128)(2,1)S(1)} %all_gather.9, f32[11264,512]{0,1:T(8,128)} %convert_element_type.33, s32[]{:T(128)S(6)} %select_n.7), kind=kOutput, calls=%fused_computation.69 | convolution fusion | flops 1479275776 | bytes 14953476 | tf_op jit(solution)/shard_map/dot_general | solution.py:78
  210.7 0.0 copy-start.2
  210.7 0.0 copy-start.4
  210.7 2.4 %copy-done.2 = f32[2816,512]{0,1:T(8,128)} copy-done((f32[2816,512]{0,1:T(8,128)}, f32[2816,512]{0,1:T(8,128)S(1)}, u32[]{:S(2)}) %copy-start.2) | copy-done | bytes 5767192
  213.2 0.6 multiply_reduce_fusion.1
  213.8 0.6 add_rsqrt_fusion.1
  214.4 0.0 copy-done.4
  214.4 0.0 copy-start.1
  214.4 7.6 %add_convert_fusion = bf16[2816,512]{0,1:T(8,128)(2,1)S(1)} fusion(f32[2816,512]{0,1:T(8,128)} %copy-done.2, bf16[512,512]{1,0:T(8,128)(2,1)} %all_gather.11, bf16[512,512]{1,0:T(8,128)(2,1)S(1)} %copy-done.4, f32[2816]{0:T(1024)} %add_rsqrt_fusion.1, f32[2816]{0:T(1024)S(1)} %broadcast_multiply_fusion.1), kind=kOutput, calls=%fused_computation.21 | convolution fusion | flops 2972975104 | bytes 9721856 | tf_op jit(solution)/shard_map/dot_general | solution.py:85
  222.0 2.7 %copy.15 = bf16[2816,512]{1,0:T(8,128)(2,1)} copy(bf16[2816,512]{0,1:T(8,128)(2,1)S(1)} %add_convert_fusion) | data formatting | bytes 5767168 | tf_op jit(solution)/shard_map/convert_element_type | solution.py:85
  224.7 0.0 copy-done.1
  (5 shorter events, 0.1 us)
Async XLA Ops:
  0.0 29.5 %copy-start = (bf16[512,128]{1,0:T(8,128)(2,1)S(1)}, bf16[512,128]{1,0:T(8,128)(2,1)}, u32[]{:S(2)}) copy-start(bf16[512,128]{1,0:T(8,128)(2,1)} %param.9) | copy-start | bytes 393220
  29.5 8.1 %copy-start.6 = (f32[64]{0:T(128)S(1)}, f32[64]{0:T(128)}, u32[]{:S(2)}) copy-start(f32[64]{0:T(128)} %param.11) | copy-start | bytes 772
  37.6 12.2 %copy-start.3 = (bf16[11264,128]{0,1:T(8,128)(2,1)}, bf16[11264,128]{0,1:T(8,128)(2,1)S(1)}, u32[]{:S(2)}) copy-start(bf16[11264,128]{0,1:T(8,128)(2,1)S(1)} %convolution_convert_fusion.1) | copy-start | bytes 8650756
  43.0 6.8 %copy-start.8 = (bf16[64,32]{0,1:T(8,128)(2,1)S(1)}, bf16[64,32]{0,1:T(8,128)(2,1)}, u32[]{:S(2)}) copy-start(bf16[64,32]{0,1:T(8,128)(2,1)} %param.10) | copy-start | bytes 12292
  52.7 30.9 %copy-start.7 = (f32[3,64,64]{2,1,0:T(8,128)S(1)}, f32[3,64,64]{2,1,0:T(8,128)}, u32[]{:S(2)}) copy-start(f32[3,64,64]{2,1,0:T(8,128)} %param.12) | copy-start | bytes 147460
  94.5 111.9 %all-to-all-start = ((bf16[4,2816,128]{1,2,0:T(8,128)(2,1)}), bf16[4,2816,128]{1,2,0:T(8,128)(2,1)S(1)}, u32[]{:S(2)}, u32[]{:S(2)}) async-start(bf16[4,2816,128]{1,2,0:T(8,128)(2,1)} %copy.13), calls=%async_computation | async-start | bytes 5767168 | tf_op jit(solution)/shard_map/all_to_all | solution.py:72
  99.4 13.0 %copy-start.5 = (bf16[128,512]{1,0:T(8,128)(2,1)S(1)}, bf16[128,512]{1,0:T(8,128)(2,1)}, u32[]{:S(2)}) copy-start(bf16[128,512]{1,0:T(8,128)(2,1)} %param.13) | copy-start | bytes 393220
  210.7 2.5 %copy-start.2 = (f32[2816,512]{0,1:T(8,128)}, f32[2816,512]{0,1:T(8,128)S(1)}, u32[]{:S(2)}) copy-start(f32[2816,512]{0,1:T(8,128)S(1)} %get-tuple-element.14) | copy-start | bytes 17301508
  210.7 3.7 %copy-start.4 = (bf16[512,512]{1,0:T(8,128)(2,1)S(1)}, bf16[512,512]{1,0:T(8,128)(2,1)}, u32[]{:S(2)}) copy-start(bf16[512,512]{1,0:T(8,128)(2,1)} %all_gather.10) | copy-start | bytes 1572868
  214.4 10.3 %copy-start.1 = (bf16[512,128]{1,0:T(8,128)(2,1)S(1)}, bf16[512,128]{1,0:T(8,128)(2,1)}, u32[]{:S(2)}) copy-start(bf16[512,128]{1,0:T(8,128)(2,1)} %param.9) | copy-start | bytes 393220
where the time goes:
time: 226 us; the launch traced here: 225 us
  blocking collectives  120 us (53%)
  matrix products  34.7 us (15%)
  local copies, waits for them, and re-layouts  33.8 us (15%)
  other arithmetic  31.3 us (14%)
  starting transfers between devices  4.87 us (2%)
    all_gather x1, blocking collectives, local(): lax.all_gather(exit_matrix, 'wid', axis=0, tiled=True)  60 us
    psum x1, blocking collectives, local(): numerator, mass = lax.psum((numerator, mass), 'pts')  25.9 us
    all_gather x1, blocking collectives, local(): lax.all_gather(widening_matrix, 'wid', axis=0, tiled=True)  17.7 us
    unnamed x19, local copies, waits for them, and re-layouts  17.3 us
    all_gather x1, blocking collectives, local(): lax.all_gather(narrowing_matrix, 'wid', axis=0, tiled=True)  16.3 us
    convert_element_type x1, other arithmetic, local(): features = vertex_features.astype(jnp.float32)  13 us
    dot_general x1, matrix products, local(): jnp.dot(normed, entry_matrix, preferred_element_type=jnp.float32)  8.08 us
    reduce_sum x2, other arithmetic, layer_norm(): variance = jnp.mean(centred * centred, axis=-1, keepdims=True)  8.01 us
  transfers between devices with their start and end apart: 1, of which 0 were waited for; matrix products, arithmetic and copies ran while one was open for 6% of the time, Pallas kernels for 0%

commit v1 on v0

v1 whole, which is shorter than its diff:
```python
import functools

import jax
import jax.numpy as jnp
from jax import lax
from jax.experimental import pallas as pl
from jax.experimental.pallas import tpu as pltpu
from jax.sharding import PartitionSpec as P

MESH = pl.DeviceIdType.MESH
F32 = jnp.float32
BF16 = jnp.bfloat16
SHARE = 2


def layer_norm(values):
    centred = values - jnp.mean(values, axis=-1, keepdims=True)
    variance = jnp.mean(centred * centred, axis=-1, keepdims=True)
    return centred * lax.rsqrt(variance + 1e-05)


def pick_tile(rows, choices):
    for choice in choices:
        if rows % choice == 0:
            return choice
    return rows


def gather_kernel(
    sizes, x_ref, ent_ref, part_ref, sharp_ref, ex_ref, up_ref, dn_ref,
    w_ref, red_ref, exg_ref, upg_ref, dng_ref,
    rows_buf, ent_buf, entt_buf, logit_mat, num_buf, mass_buf,
    piece_all, piece_in, piece_sum, ring_in, fin_buf,
    x_sem, own_sem, zs_sem, zr_sem, fs_sem, fr_sem,
    rs_send, rs_recv, z_send, z_recv, ag_send, ag_recv,
):
    pts, wid, share, tile, head, slices, heads = sizes
    p, w = lax.axis_index("pts"), lax.axis_index("wid")
    rows = rows_buf.shape[0]
    tiles = rows // tile
    group, member = p // share, p % share

    x_copy = pltpu.make_async_copy(
        x_ref.at[pl.ds(pl.multiple_of(w * rows, rows), rows)], rows_buf, x_sem
    )
    x_copy.start()

    barrier = pltpu.get_barrier_semaphore()
    for d in range(1, wid):
        pl.semaphore_signal(
            barrier, inc=1, device_id=(p, lax.rem(w + d, wid)), device_id_type=MESH
        )
    for d in range(1, pts):
        pl.semaphore_signal(
            barrier, inc=1, device_id=(lax.rem(p + d, pts), w), device_id_type=MESH
        )
    pl.semaphore_wait(barrier, wid - 1 + pts - 1)

    chunk = ex_ref.shape[0]
    ent_part = ent_ref.shape[0] // share
    out_part = chunk // share

    def spot(m, owner, part):
        if m == 0:
            return ent_buf.at[owner, pl.ds(pl.multiple_of(part * ent_part, ent_part), ent_part)]
        full = (exg_ref, upg_ref, dng_ref)[m - 1]
        return full.at[pl.ds(pl.multiple_of(owner * chunk + part * out_part, out_part), out_part)]

    def mine(m):
        if m == 0:
            return ent_ref.at[pl.ds(pl.multiple_of(member * ent_part, ent_part), ent_part)]
        own = (ex_ref, up_ref, dn_ref)[m - 1]
        return own.at[pl.ds(pl.multiple_of(member * out_part, out_part), out_part)]

    def across(m, d):
        return pltpu.make_async_remote_copy(
            src_ref=mine(m), dst_ref=spot(m, w, member),
            send_sem=zs_sem.at[m, d - 1], recv_sem=zr_sem.at[m, d - 1],
            device_id=(p, lax.rem(w + d, wid)), device_id_type=MESH,
        )

    def forward(m, d, e):
        owner = lax.rem(w - d + wid, wid)
        return pltpu.make_async_remote_copy(
            src_ref=spot(m, owner, member), dst_ref=spot(m, owner, member),
            send_sem=fs_sem.at[m, d - 1, e - 1], recv_sem=fr_sem.at[m, d - 1, e - 1],
            device_id=(group * share + lax.rem(member + e, share), w), device_id_type=MESH,
        )

    crossing = [[across(m, d) for d in range(1, wid)] for m in range(4)]
    for m in range(4):
        for copy in crossing[m]:
            copy.start()
    own_copies = []
    for m in range(1, 4):
        full = (exg_ref, upg_ref, dng_ref)[m - 1]
        copy = pltpu.make_async_copy(
            (ex_ref, up_ref, dn_ref)[m - 1],
            full.at[pl.ds(pl.multiple_of(w * chunk, chunk), chunk)], own_sem.at[m - 1],
        )
        copy.start()
        own_copies.append(copy)

    held = logit_mat.shape[1] // head
    wide = held * slices
    logit_mat[...] = jnp.zeros_like(logit_mat)
    part_t = part_ref[...].astype(F32).T
    sharp = sharp_ref[...]
    sharp_hi = sharp.astype(BF16).astype(F32)
    sharp_lo = sharp - sharp_hi
    for h in range(held):
        lanes = slice(h * head, (h + 1) * head)
        logit_mat[h * slices:(h + 1) * slices, lanes] = part_t
        logit_mat[wide + h:wide + h + 1, lanes] = sharp_hi
        logit_mat[wide + 8 + h:wide + 8 + h + 1, lanes] = sharp_lo
    num_buf[...] = jnp.zeros_like(num_buf)
    mass_buf[...] = jnp.zeros_like(mass_buf)
    x_copy.wait()

    def norm_step(t, carry):
        at = pl.ds(pl.multiple_of(t * tile, tile), tile)
        rows_buf[at, :] = layer_norm(rows_buf[at, :].astype(F32)).astype(BF16)
        return carry

    lax.fori_loop(0, tiles, norm_step, 0)

    def pass_on(m):
        copies = []
        for d in range(1, wid):
            crossing[m][d - 1].wait_recv()
            for e in range(1, share):
                copy = forward(m, d, e)
                copy.start()
                copies.append(copy)
        return copies

    width = ent_ref.shape[1]
    passed = [pass_on(0)]
    for copy in passed[0]:
        copy.wait_recv()
    own_at = pl.ds(pl.multiple_of(w * width, width), width)
    entt_buf[own_at, :] = ent_ref[...].T
    for d in range(1, wid):
        owner = lax.rem(w - d + wid, wid)
        entt_buf[pl.ds(pl.multiple_of(owner * width, width), width), :] = ent_buf[owner].T

    lhs = logit_mat[...].astype(BF16)
    groups = heads // held
    both = (((1,), (1,)), ((), ()))

    def slice_step(t, carry):
        at = pl.ds(pl.multiple_of(t * tile, tile), tile)
        feats = lax.dot_general(
            entt_buf[...], rows_buf[at, :], both, preferred_element_type=F32
        ).astype(BF16)
        for gi in range(groups):
            own = feats[gi * held * head:(gi + 1) * held * head]
            logits = jnp.dot(lhs, own, preferred_element_type=F32)
            raw = logits[wide:wide + 8] + logits[wide + 8:wide + 16]
            soft = jnp.maximum(raw, 0.0) + jnp.log1p(jnp.exp(-jnp.abs(raw)))
            inverse = 1.0 / (0.5 + soft)
            weights = []
            for h in range(held):
                score = logits[h * slices:(h + 1) * slices] * inverse[h:h + 1]
                power = jnp.exp(score - jnp.max(score, axis=0, keepdims=True))
                weights.append(power * (1.0 / jnp.sum(power, axis=0, keepdims=True)))
            block = jnp.concatenate(weights, axis=0).astype(BF16)
            num_buf[gi] += lax.dot_general(block, own, both, preferred_element_type=F32)
            rounded = block.astype(F32)
            mass = rounded[:, :128]
            for c in range(1, tile // 128):
                mass = mass + rounded[:, c * 128:(c + 1) * 128]
            mass_buf[gi * wide:(gi + 1) * wide] += mass
            w_ref[at, gi * wide:(gi + 1) * wide] = block.T
        return carry

    lax.fori_loop(0, tiles, slice_step, 0)

    lane = lax.broadcasted_iota(jnp.int32, (slices, 2 * head), 1)
    for h in range(heads):
        gi, k = h // held, h % held
        block = num_buf[gi, k * slices:(k + 1) * slices, (k // 2) * 2 * head:(k // 2 + 1) * 2 * head]
        if k % 2:
            block = pltpu.roll(block, head, 1)
        mass = jnp.sum(mass_buf[h * slices:(h + 1) * slices], axis=1, keepdims=True)
        piece_all[h * slices:(h + 1) * slices] = jnp.where(lane < head, block, mass)

    size = heads * slices // pts

    def piece(ref, owner):
        return ref.at[pl.ds(pl.multiple_of(owner * size, size), size)]

    scatter = []
    for d in range(1, pts):
        to = lax.rem(p + d, pts)
        scatter.append(pltpu.make_async_remote_copy(
            src_ref=piece(piece_all, to), dst_ref=piece_in.at[d - 1],
            send_sem=rs_send.at[d - 1], recv_sem=rs_recv.at[d - 1],
            device_id=(to, w), device_id_type=MESH,
        ))
    for copy in scatter:
        copy.start()
    passed += [pass_on(m) for m in range(1, 4)]
    total = piece_all[pl.ds(pl.multiple_of(p * size, size), size)]
    for d in range(1, pts):
        scatter[d - 1].wait_recv()
        total = total + piece_in[d - 1]
    piece_sum[...] = total
    ring = []
    for d in range(1, wid):
        ring.append(pltpu.make_async_remote_copy(
            src_ref=piece_sum, dst_ref=ring_in.at[d - 1],
            send_sem=z_send.at[d - 1], recv_sem=z_recv.at[d - 1],
            device_id=(p, lax.rem(w + d, wid)), device_id_type=MESH,
        ))
    for copy in ring:
        copy.start()
    for d in range(1, wid):
        ring[d - 1].wait_recv()
        total = total + ring_in[d - 1]
    fin_buf[pl.ds(pl.multiple_of(p * size, size), size)] = total
    spread = []
    for d in range(1, pts):
        spread.append(pltpu.make_async_remote_copy(
            src_ref=piece(fin_buf, p), dst_ref=piece(fin_buf, p),
            send_sem=ag_send.at[d - 1], recv_sem=ag_recv.at[d - 1],
            device_id=(lax.rem(p + d, pts), w), device_id_type=MESH,
        ))
    for copy in spread:
        copy.start()
    for copy in spread:
        copy.wait_recv()
    red_ref[...] = fin_buf[...]
    for m in range(1, 4):
        for copy in passed[m]:
            copy.wait_recv()
    for copy in own_copies:
        copy.wait()
    for copies in crossing + passed + [scatter, ring, spread]:
        for copy in copies:
            copy.wait_send()


def rows_kernel(
    sizes, at_ref, red_ref, qkv_ref, w_ref, x_ref, exg_ref, upg_ref, dng_ref, out_ref, mix_buf
):
    head, slices, heads = sizes

    @pl.when(pl.program_id(0) == 0)
    def _():
        high = lax.Precision.HIGHEST
        count = heads * slices
        red = red_ref[...]
        tokens = red[:, :head] / (red[:, head:] + 1e-05)
        queries, keys_all, value_rows = (
            jnp.dot(tokens, qkv_ref[i], precision=high, preferred_element_type=F32)
            for i in range(3)
        )
        scores = lax.dot_general(
            queries, keys_all, (((1,), (1,)), ((), ())), precision=high,
            preferred_element_type=F32,
        ) * (1.0 / head ** 0.5)
        row = lax.broadcasted_iota(jnp.int32, (count, count), 0) // slices
        col = lax.broadcasted_iota(jnp.int32, (count, count), 1) // slices
        scores = jnp.where(row == col, scores, -jnp.inf)
        power = jnp.exp(scores - jnp.max(scores, axis=1, keepdims=True))
        attend = power / jnp.sum(power, axis=1, keepdims=True)
        out_tok = jnp.dot(attend, value_rows, precision=high, preferred_element_type=F32)
        spread = jnp.concatenate([out_tok] * heads, axis=1)
        row = lax.broadcasted_iota(jnp.int32, spread.shape, 0) // slices
        col = lax.broadcasted_iota(jnp.int32, spread.shape, 1) // head
        spread = jnp.where(row == col, spread, 0.0).astype(BF16)
        mix_buf[...] = jnp.dot(
            spread, exg_ref[...], preferred_element_type=F32
        ).astype(BF16)

    midway = x_ref[...].astype(F32) + jnp.dot(
        w_ref[...], mix_buf[...], preferred_element_type=F32
    )
    normed = layer_norm(midway).astype(BF16)
    hidden = jax.nn.gelu(jnp.dot(normed, upg_ref[...], preferred_element_type=F32)).astype(BF16)
    out_ref[...] = (
        midway + jnp.dot(hidden, dng_ref[...], preferred_element_type=F32)
    ).astype(BF16)


def local(x, entry, partition, sharpness, qkv, exit_m, widening, narrowing):
    pts, wid = lax.axis_size("pts"), lax.axis_size("wid")
    width = x.shape[1]
    head, slices = partition.shape
    heads = entry.shape[1] * wid // head
    rows = x.shape[0] // wid
    chunk = exit_m.shape[0]
    cells = heads * slices
    tile = pick_tile(rows, (256, 128))
    held = 256 // head
    size = cells // pts
    share = SHARE
    sizes = (pts, wid, share, tile, head, slices, heads)
    vmem = pl.BlockSpec(memory_space=pltpu.VMEM)
    hbm = pl.BlockSpec(memory_space=pl.ANY)
    dma = pltpu.SemaphoreType.DMA
    full = jax.ShapeDtypeStruct((chunk * wid, width), BF16)
    weights, reduced, exg, upg, dng = pl.pallas_call(
        functools.partial(gather_kernel, sizes),
        name="slices_and_gather",
        out_shape=(
            jax.ShapeDtypeStruct((rows, cells), BF16),
            jax.ShapeDtypeStruct((cells, 2 * head), F32),
            full, full, full,
        ),
        in_specs=[hbm] + [vmem] * 6,
        out_specs=(vmem, vmem, hbm, hbm, hbm),
        scratch_shapes=[
            pltpu.VMEM((rows, width), BF16),
            pltpu.VMEM((wid,) + entry.shape, BF16),
            pltpu.VMEM((entry.shape[1] * wid, entry.shape[0]), BF16),
            pltpu.VMEM((held * slices + 16, held * head), F32),
            pltpu.VMEM((heads // held, held * slices, held * head), F32),
            pltpu.VMEM((cells, 128), F32),
            pltpu.VMEM((cells, 2 * head), F32),
            pltpu.VMEM((pts - 1, size, 2 * head), F32),
            pltpu.VMEM((size, 2 * head), F32),
            pltpu.VMEM((wid - 1, size, 2 * head), F32),
            pltpu.VMEM((cells, 2 * head), F32),
            dma, dma((3,)),
            dma((4, wid - 1)), dma((4, wid - 1)),
            dma((4, wid - 1, share - 1)), dma((4, wid - 1, share - 1)),
            dma((pts - 1,)), dma((pts - 1,)),
            dma((wid - 1,)), dma((wid - 1,)),
            dma((pts - 1,)), dma((pts - 1,)),
        ],
        compiler_params=pltpu.CompilerParams(
            collective_id=0, has_side_effects=True, vmem_limit_bytes=40 * 1024 * 1024
        ),
    )(x, entry, partition, sharpness.reshape(1, head), exit_m, widening, narrowing)

    step = pick_tile(rows, (704, 256, 128))
    steps = rows // step
    whole = lambda a: pl.BlockSpec(a.shape, lambda i, at: (0,) * a.ndim)
    at = lax.axis_index("wid").astype(jnp.int32).reshape(1)
    return pl.pallas_call(
        functools.partial(rows_kernel, (head, slices, heads)),
        name="mix_and_feed",
        out_shape=jax.ShapeDtypeStruct((rows, width), BF16),
        grid_spec=pltpu.PrefetchScalarGridSpec(
            num_scalar_prefetch=1,
            grid=(steps,),
            in_specs=[
                whole(reduced),
                whole(qkv),
                pl.BlockSpec((step, cells), lambda i, at: (i, 0)),
                pl.BlockSpec((step, width), lambda i, at: (at[0] * steps + i, 0)),
                whole(exg), whole(upg), whole(dng),
            ],
            out_specs=pl.BlockSpec((step, width), lambda i, at: (i, 0)),
            scratch_shapes=[pltpu.VMEM((cells, width), BF16)],
        ),
        compiler_params=pltpu.CompilerParams(
            dimension_semantics=("arbitrary",), vmem_limit_bytes=48 * 1024 * 1024
        ),
    )(at, reduced, qkv, weights, x, exg, upg, dng)


def solution(mesh):
    placed = (
        P("pts", None),
        P(None, "wid"),
        P(),
        P(),
        P(),
        P("wid", None),
        P("wid", None),
        P("wid", None),
    )
    return jax.shard_map(
        local, mesh=mesh, in_specs=placed, out_specs=P(("pts", "wid"), None), check_vma=False
    )
```

time: 226 us -> 55 us (0.24)
  blocking collectives: 120 us -> 0 us
  Pallas kernels: 0 us -> 49.7 us
  matrix products: 34.7 us -> 0 us
  other arithmetic: 31.3 us -> 0 us
  local copies, waits for them, and re-layouts: 33.8 us -> 5.06 us
  starting transfers between devices: 4.87 us -> 0 us
    all_gather x3 -> x0, blocking collectives: 94 us -> none  [the longest x1 60 us: local(): lax.all_gather(exit_matrix, 'wid', axis=0, tiled=True)]
    pallas_call x0 -> x2, Pallas kernels: none -> 49.7 us  [the longest x1 39.1 us: local(): pl.pallas_call(functools.partial(gather_kernel, sizes), name='slices_and_...]
    dot_general x11 -> x0, matrix products: 31.7 us -> none  [the longest x1 8.08 us: local(): jnp.dot(normed, entry_matrix, preferred_element_type=jnp.float32)]
    psum x1 -> x0, blocking collectives: 25.9 us -> none  [local(): numerator, mass = lax.psum((numerator, mass), 'pts')]
    reduce_sum x5 -> x0, other arithmetic: 17.5 us -> none  [the longest x2 8.01 us: layer_norm(): variance = jnp.mean(centred * centred, axis=-1, keepdims=True)]
    convert_element_type x1 -> x0, other arithmetic: 13 us -> none  [local(): features = vertex_features.astype(jnp.float32)]
    unnamed x19 -> x13, local copies, waits for them, and re-layouts: 17.3 us -> 5.06 us
    all_to_all x2 -> x0, local copies, waits for them, and re-layouts: 7.14 us -> none  [local(): lax.all_to_all(deslice, 'wid', split_axis=0, concat_axis=1, tiled=True)]
  transfers between devices with their start and end apart: 1 -> 0, of which waited for: 0 -> 0; matrix products, arithmetic and copies ran while one was open for 6% -> 0% of each run, Pallas kernels for 0% -> 0%
where the time goes in v1:
time: 55 us; the launch traced here: 54.8 us
  Pallas kernels  49.7 us (90%)
  local copies, waits for them, and re-layouts  5.06 us (9%)
    pallas_call x1, Pallas kernels, local(): pl.pallas_call(functools.partial(gather_kernel, sizes), name='slices_and_...  39.1 us
    pallas_call x1, Pallas kernels, local(): pl.pallas_call(functools.partial(rows_kernel, (head, slices, heads)), nam...  10.6 us
    unnamed x13, local copies, waits for them, and re-layouts  5.06 us

profile of v1, /device:TPU:0, one launch (start us, length us, event | category | flops | bytes accessed | tf_op | source)
XLA Modules:
  0.0 54.8 jit_solution(3872753498164170405)
XLA Ops:
  0.0 0.8 %copy.9.part_ref = bf16[64,32]{1,0:T(8,128)(2,1)S(1)} copy(bf16[64,32]{0,1:T(8,128)(2,1)} %param.10) | data formatting | bytes 8192 | tf_op args[2]
  0.8 0.0 copy-start
  0.8 0.9 %copy-done = bf16[512,128]{1,0:T(8,128)(2,1)S(1)} copy-done((bf16[512,128]{1,0:T(8,128)(2,1)S(1)}, bf16[512,128]{1,0:T(8,128)(2,1)}, u32[]{:S(2)}) %copy-start) | copy-done | bytes 131096
  1.7 0.0 copy-start.1
  1.7 0.9 %copy-done.1 = bf16[128,512]{1,0:T(8,128)(2,1)S(1)} copy-done((bf16[128,512]{1,0:T(8,128)(2,1)S(1)}, bf16[128,512]{1,0:T(8,128)(2,1)}, u32[]{:S(2)}) %copy-start.1) | copy-done | bytes 131096
  2.6 0.0 copy-start.2
  2.6 0.9 %copy-done.2 = bf16[128,512]{1,0:T(8,128)(2,1)S(1)} copy-done((bf16[128,512]{1,0:T(8,128)(2,1)S(1)}, bf16[128,512]{1,0:T(8,128)(2,1)}, u32[]{:S(2)}) %copy-start.2) | copy-done | bytes 131096
  3.5 0.0 copy-start.3
  3.5 0.9 %copy-done.3 = bf16[128,512]{1,0:T(8,128)(2,1)S(1)} copy-done((bf16[128,512]{1,0:T(8,128)(2,1)S(1)}, bf16[128,512]{1,0:T(8,128)(2,1)}, u32[]{:S(2)}) %copy-start.3) | copy-done | bytes 131096
  4.4 0.0 copy-start.5
  4.4 0.7 %copy-done.5 = f32[64]{0:T(128)S(1)} copy-done((f32[64]{0:T(128)S(1)}, f32[64]{0:T(128)}, u32[]{:S(2)}) %copy-start.5) | copy-done | bytes 280
  5.1 0.0 copy-start.4
  5.1 39.1 %slices_and_gather.1 = (bf16[2816,256]{1,0:T(8,128)(2,1)S(1)}, f32[256,128]{1,0:T(8,128)S(1)}, bf16[512,512]{1,0:T(8,128)(2,1)S(1)}, bf16[512,512]{1,0:T(8,128)(2,1)S(1)}, bf16[512,512]{1,0:T(8,128)(2,1)S(1)}) custom-call(bf16[11264,512]{1,0:T(8,128)(2,1)} %x_ref.3, bf16[512,128]{1,0:T(8,128)(2,1)S(1)} %copy-done, bf16[64,32]{1,0:T(8,128)(2,1)S(1)} %copy.9.part_ref, ...), custom_call_target="tpu_custom_call" | custom-call | tf_op jit(solution)/shard_map/slices_and_gather/pallas_call | solution.py:304
  44.2 0.0 copy-done.4
  44.2 10.6 %mix_and_feed.1 = bf16[2816,512]{1,0:T(8,128)(2,1)} custom-call(s32[1]{0:T(128)} %bitcast.at_ref, f32[256,128]{1,0:T(8,128)S(1)} %get-tuple-element.10.red_ref, f32[3,64,64]{2,1,0:T(8,128)S(1)} %copy-done.4, bf16[2816,256]{1,0:T(8,128)(2,1)S(1)} %get-tuple-element.11.w_ref, bf16[11264,512]{1,0:T(8,128)(2,1)} %x_ref.3, ...), custom_call_target="tpu_custom_call" | custom-call | tf_op jit(solution)/shard_map/mix_and_feed/pallas_call | solution.py:342
Async XLA Ops:
  0.8 0.9 %copy-start = (bf16[512,128]{1,0:T(8,128)(2,1)S(1)}, bf16[512,128]{1,0:T(8,128)(2,1)}, u32[]{:S(2)}) copy-start(bf16[512,128]{1,0:T(8,128)(2,1)} %ent_ref.1) | copy-start | bytes 393220
  1.7 0.9 %copy-start.1 = (bf16[128,512]{1,0:T(8,128)(2,1)S(1)}, bf16[128,512]{1,0:T(8,128)(2,1)}, u32[]{:S(2)}) copy-start(bf16[128,512]{1,0:T(8,128)(2,1)} %ex_ref.1) | copy-start | bytes 393220
  2.6 0.9 %copy-start.2 = (bf16[128,512]{1,0:T(8,128)(2,1)S(1)}, bf16[128,512]{1,0:T(8,128)(2,1)}, u32[]{:S(2)}) copy-start(bf16[128,512]{1,0:T(8,128)(2,1)} %up_ref.1) | copy-start | bytes 393220
  3.5 0.9 %copy-start.3 = (bf16[128,512]{1,0:T(8,128)(2,1)S(1)}, bf16[128,512]{1,0:T(8,128)(2,1)}, u32[]{:S(2)}) copy-start(bf16[128,512]{1,0:T(8,128)(2,1)} %dn_ref.1) | copy-start | bytes 393220
  4.4 0.7 %copy-start.5 = (f32[64]{0:T(128)S(1)}, f32[64]{0:T(128)}, u32[]{:S(2)}) copy-start(f32[64]{0:T(128)} %param.11) | copy-start | bytes 772
  5.1 39.1 %copy-start.4 = (f32[3,64,64]{2,1,0:T(8,128)S(1)}, f32[3,64,64]{2,1,0:T(8,128)}, u32[]{:S(2)}) copy-start(f32[3,64,64]{2,1,0:T(8,128)} %qkv_ref.1) | copy-start | bytes 147460

commit v2 on v1

--- a/solution.py
+++ b/solution.py
@@ -10,7 +10,6 @@
 MESH = pl.DeviceIdType.MESH
 F32 = jnp.float32
 BF16 = jnp.bfloat16
-SHARE = 2
 
 
 def layer_norm(values):
@@ -27,24 +26,37 @@
 
 
 def gather_kernel(
-    sizes, x_ref, ent_ref, part_ref, sharp_ref, ex_ref, up_ref, dn_ref,
+    sizes, x_ref, ent_ref, part_hbm, sharp_hbm, ex_ref, up_ref, dn_ref,
     w_ref, red_ref, exg_ref, upg_ref, dng_ref,
     rows_buf, ent_buf, entt_buf, logit_mat, num_buf, mass_buf,
-    piece_all, piece_in, piece_sum, ring_in, fin_buf,
-    x_sem, own_sem, zs_sem, zr_sem, fs_sem, fr_sem,
+    piece_all, piece_in, piece_sum, ring_in, fin_buf, part_ref, sharp_ref,
+    x_sem, own_sem, zs_sem, zr_sem, fs_sem, fr_sem, cs_sem, cr_sem,
     rs_send, rs_recv, z_send, z_recv, ag_send, ag_recv,
 ):
     pts, wid, share, tile, head, slices, heads = sizes
     p, w = lax.axis_index("pts"), lax.axis_index("wid")
     rows = rows_buf.shape[0]
     tiles = rows // tile
-    group, member = p // share, p % share
+    norm_tile = pick_tile(rows, (704, 256, 128))
+    norm_tiles = rows // norm_tile
+    chips = share // 2
+    group, core = p // share, p % 2
+    chip = (p % share) // 2
+    member = core * chips + chip
 
     x_copy = pltpu.make_async_copy(
         x_ref.at[pl.ds(pl.multiple_of(w * rows, rows), rows)], rows_buf, x_sem
     )
     x_copy.start()
 
+    small_copies = [
+        pltpu.make_async_copy(part_hbm, part_ref, own_sem.at[0]),
+        pltpu.make_async_copy(sharp_hbm, sharp_ref, own_sem.at[1]),
+        pltpu.make_async_copy(ent_ref, ent_buf.at[w], own_sem.at[2]),
+    ]
+    for copy in small_copies:
+        copy.start()
+
     barrier = pltpu.get_barrier_semaphore()
     for d in range(1, wid):
         pl.semaphore_signal(
@@ -60,15 +72,17 @@
     ent_part = ent_ref.shape[0] // share
     out_part = chunk // share
 
-    def spot(m, owner, part):
+    def spot(m, owner, part, parts=1):
         if m == 0:
-            return ent_buf.at[owner, pl.ds(pl.multiple_of(part * ent_part, ent_part), ent_part)]
+            count = ent_part * parts
+            return ent_buf.at[owner, pl.ds(pl.multiple_of(part * count, count), count)]
+        count = out_part * parts
         full = (exg_ref, upg_ref, dng_ref)[m - 1]
-        return full.at[pl.ds(pl.multiple_of(owner * chunk + part * out_part, out_part), out_part)]
+        return full.at[pl.ds(pl.multiple_of(owner * chunk + part * count, count), count)]
 
     def mine(m):
         if m == 0:
-            return ent_ref.at[pl.ds(pl.multiple_of(member * ent_part, ent_part), ent_part)]
+            return spot(0, w, member)
         own = (ex_ref, up_ref, dn_ref)[m - 1]
         return own.at[pl.ds(pl.multiple_of(member * out_part, out_part), out_part)]
 
@@ -81,12 +95,23 @@
 
     def forward(m, d, e):
         owner = lax.rem(w - d + wid, wid)
+        to = group * share + 2 * lax.rem(chip + e, chips) + core
         return pltpu.make_async_remote_copy(
             src_ref=spot(m, owner, member), dst_ref=spot(m, owner, member),
             send_sem=fs_sem.at[m, d - 1, e - 1], recv_sem=fr_sem.at[m, d - 1, e - 1],
-            device_id=(group * share + lax.rem(member + e, share), w), device_id_type=MESH,
-        )
-
+            device_id=(to, w), device_id_type=MESH,
+        )
+
+    def swap(m, d):
+        owner = lax.rem(w - d + wid, wid)
+        half = spot(m, owner, core, chips)
+        return pltpu.make_async_remote_copy(
+            src_ref=half, dst_ref=half,
+            send_sem=cs_sem.at[m, d - 1], recv_sem=cr_sem.at[m, d - 1],
+            device_id=(p + 1 - 2 * core, w), device_id_type=MESH,
+        )
+
+    small_copies[2].wait()
     crossing = [[across(m, d) for d in range(1, wid)] for m in range(4)]
     for m in range(4):
         for copy in crossing[m]:
@@ -96,7 +121,7 @@
         full = (exg_ref, upg_ref, dng_ref)[m - 1]
         copy = pltpu.make_async_copy(
             (ex_ref, up_ref, dn_ref)[m - 1],
-            full.at[pl.ds(pl.multiple_of(w * chunk, chunk), chunk)], own_sem.at[m - 1],
+            full.at[pl.ds(pl.multiple_of(w * chunk, chunk), chunk)], own_sem.at[m + 2],
         )
         copy.start()
         own_copies.append(copy)
@@ -104,7 +129,9 @@
     held = logit_mat.shape[1] // head
     wide = held * slices
     logit_mat[...] = jnp.zeros_like(logit_mat)
-    part_t = part_ref[...].astype(F32).T
+    for copy in small_copies[:2]:
+        copy.wait()
+    part_t = part_ref[...].astype(F32)
     sharp = sharp_ref[...]
     sharp_hi = sharp.astype(BF16).astype(F32)
     sharp_lo = sharp - sharp_hi
@@ -118,29 +145,41 @@
     x_copy.wait()
 
     def norm_step(t, carry):
-        at = pl.ds(pl.multiple_of(t * tile, tile), tile)
+        at = pl.ds(pl.multiple_of(t * norm_tile, norm_tile), norm_tile)
         rows_buf[at, :] = layer_norm(rows_buf[at, :].astype(F32)).astype(BF16)
         return carry
 
-    lax.fori_loop(0, tiles, norm_step, 0)
+    norm_way = norm_tiles // 2
+    lax.fori_loop(0, norm_way, norm_step, 0)
 
     def pass_on(m):
         copies = []
         for d in range(1, wid):
             crossing[m][d - 1].wait_recv()
-            for e in range(1, share):
+            for e in range(1, chips):
                 copy = forward(m, d, e)
                 copy.start()
                 copies.append(copy)
         return copies
 
+    def trade(m):
+        copies = []
+        for d in range(1, wid):
+            for e in range(1, chips):
+                passed[m][(d - 1) * (chips - 1) + e - 1].wait_recv()
+            copy = swap(m, d)
+            copy.start()
+            copies.append(copy)
+        return copies
+
     width = ent_ref.shape[1]
     passed = [pass_on(0)]
-    for copy in passed[0]:
+    lax.fori_loop(norm_way, norm_tiles, norm_step, 0)
+    traded = [trade(0)]
+    passed += [pass_on(m) for m in range(1, 4)]
+    for copy in traded[0]:
         copy.wait_recv()
-    own_at = pl.ds(pl.multiple_of(w * width, width), width)
-    entt_buf[own_at, :] = ent_ref[...].T
-    for d in range(1, wid):
+    for d in range(wid):
         owner = lax.rem(w - d + wid, wid)
         entt_buf[pl.ds(pl.multiple_of(owner * width, width), width), :] = ent_buf[owner].T
 
@@ -174,7 +213,10 @@
             w_ref[at, gi * wide:(gi + 1) * wide] = block.T
         return carry
 
-    lax.fori_loop(0, tiles, slice_step, 0)
+    part_way = (tiles + 1) // 2
+    lax.fori_loop(0, part_way, slice_step, 0)
+    traded += [trade(m) for m in range(1, 4)]
+    lax.fori_loop(part_way, tiles, slice_step, 0)
 
     lane = lax.broadcasted_iota(jnp.int32, (slices, 2 * head), 1)
     for h in range(heads):
@@ -200,7 +242,6 @@
         ))
     for copy in scatter:
         copy.start()
-    passed += [pass_on(m) for m in range(1, 4)]
     total = piece_all[pl.ds(pl.multiple_of(p * size, size), size)]
     for d in range(1, pts):
         scatter[d - 1].wait_recv()
@@ -232,11 +273,11 @@
         copy.wait_recv()
     red_ref[...] = fin_buf[...]
     for m in range(1, 4):
-        for copy in passed[m]:
+        for copy in traded[m]:
             copy.wait_recv()
     for copy in own_copies:
         copy.wait()
-    for copies in crossing + passed + [scatter, ring, spread]:
+    for copies in crossing + passed + traded + [scatter, ring, spread]:
         for copy in copies:
             copy.wait_send()
 
@@ -292,13 +333,18 @@
     rows = x.shape[0] // wid
     chunk = exit_m.shape[0]
     cells = heads * slices
-    tile = pick_tile(rows, (256, 128))
+    tile = pick_tile(rows, (1408, 256, 128))
     held = 256 // head
     size = cells // pts
-    share = SHARE
+    share = 2
+    for choice in (8, 4):
+        if pts % choice == 0 and chunk % (16 * choice) == 0:
+            share = choice
+            break
     sizes = (pts, wid, share, tile, head, slices, heads)
     vmem = pl.BlockSpec(memory_space=pltpu.VMEM)
-    hbm = pl.BlockSpec(memory_space=pl.ANY)
+    hbm = pl.BlockSpec(memory_space=pltpu.HBM)
+    anywhere = pl.BlockSpec(memory_space=pl.ANY)
     dma = pltpu.SemaphoreType.DMA
     full = jax.ShapeDtypeStruct((chunk * wid, width), BF16)
     weights, reduced, exg, upg, dng = pl.pallas_call(
@@ -309,8 +355,8 @@
             jax.ShapeDtypeStruct((cells, 2 * head), F32),
             full, full, full,
         ),
-        in_specs=[hbm] + [vmem] * 6,
-        out_specs=(vmem, vmem, hbm, hbm, hbm),
+        in_specs=[hbm] * 7,
+        out_specs=(vmem, vmem, anywhere, anywhere, anywhere),
         scratch_shapes=[
             pltpu.VMEM((rows, width), BF16),
             pltpu.VMEM((wid,) + entry.shape, BF16),
@@ -323,19 +369,22 @@
             pltpu.VMEM((size, 2 * head), F32),
             pltpu.VMEM((wid - 1, size, 2 * head), F32),
             pltpu.VMEM((cells, 2 * head), F32),
-            dma, dma((3,)),
+            pltpu.VMEM((slices, head), BF16),
+            pltpu.VMEM((1, head), F32),
+            dma, dma((6,)),
             dma((4, wid - 1)), dma((4, wid - 1)),
-            dma((4, wid - 1, share - 1)), dma((4, wid - 1, share - 1)),
+            dma((4, wid - 1, max(share // 2 - 1, 1))), dma((4, wid - 1, max(share // 2 - 1, 1))),
+            dma((4, wid - 1)), dma((4, wid - 1)),
             dma((pts - 1,)), dma((pts - 1,)),
             dma((wid - 1,)), dma((wid - 1,)),
             dma((pts - 1,)), dma((pts - 1,)),
         ],
         compiler_params=pltpu.CompilerParams(
-            collective_id=0, has_side_effects=True, vmem_limit_bytes=40 * 1024 * 1024
+            collective_id=0, has_side_effects=True, vmem_limit_bytes=60 * 1024 * 1024
         ),
-    )(x, entry, partition, sharpness.reshape(1, head), exit_m, widening, narrowing)
-
-    step = pick_tile(rows, (704, 256, 128))
+    )(x, entry, partition.T, sharpness.reshape(1, head), exit_m, widening, narrowing)
+
+    step = pick_tile(rows, (1408, 704, 256, 128))
     steps = rows // step
     whole = lambda a: pl.BlockSpec(a.shape, lambda i, at: (0,) * a.ndim)
     at = lax.axis_index("wid").astype(jnp.int32).reshape(1)
@@ -357,7 +406,7 @@
             scratch_shapes=[pltpu.VMEM((cells, width), BF16)],
         ),
         compiler_params=pltpu.CompilerParams(
-            dimension_semantics=("arbitrary",), vmem_limit_bytes=48 * 1024 * 1024
+            dimension_semantics=("arbitrary",), vmem_limit_bytes=61 * 1024 * 1024
         ),
     )(at, reduced, qkv, weights, x, exg, upg, dng)
 

time: 55 us -> 46.8 us (0.85)
  local copies, waits for them, and re-layouts: 5.06 us -> 0 us
  Pallas kernels: 49.7 us -> 46.6 us
    unnamed x13 -> x0, local copies, waits for them, and re-layouts: 5.06 us -> none
    pallas_call x1, Pallas kernels: 39.1 us -> 35.9 us  [local(): pl.pallas_call(functools.partial(gather_kernel, sizes), name='slices_and_...]
where the time goes in v2:
time: 46.8 us; the launch traced here: 46.6 us
  Pallas kernels  46.6 us (100%)
    pallas_call x1, Pallas kernels, local(): pl.pallas_call(functools.partial(gather_kernel, sizes), name='slices_and_...  35.9 us
    pallas_call x1, Pallas kernels, local(): pl.pallas_call(functools.partial(rows_kernel, (head, slices, heads)), nam...  10.7 us

profile of v2, /device:TPU:0, one launch (start us, length us, event | category | flops | bytes accessed | tf_op | source)
XLA Modules:
  0.0 46.6 jit_solution(12244394268707064452)
XLA Ops:
  0.0 35.9 %slices_and_gather.1 = (bf16[2816,256]{1,0:T(8,128)(2,1)}, f32[256,128]{1,0:T(8,128)}, bf16[512,512]{1,0:T(8,128)(2,1)}, bf16[512,512]{1,0:T(8,128)(2,1)}, bf16[512,512]{1,0:T(8,128)(2,1)}) custom-call(bf16[11264,512]{1,0:T(8,128)(2,1)} %x_ref.3, bf16[512,128]{1,0:T(8,128)(2,1)} %ent_ref.1, bf16[32,64]{1,0:T(8,128)(2,1)} %bitcast.3, f32[1,64]{1,0:T(1,128)} %bitcast.4, ...), custom_call_target="tpu_custom_call" | custom-call | tf_op jit(solution)/shard_map/slices_and_gather/pallas_call | solution.py:350
  36.0 10.7 %mix_and_feed.1 = bf16[2816,512]{1,0:T(8,128)(2,1)} custom-call(s32[1]{0:T(128)} %bitcast.at_ref, f32[256,128]{1,0:T(8,128)} %get-tuple-element.10.red_ref, f32[3,64,64]{2,1,0:T(8,128)} %qkv_ref.1, bf16[2816,256]{1,0:T(8,128)(2,1)} %get-tuple-element.11.w_ref, bf16[11264,512]{1,0:T(8,128)(2,1)} %x_ref.3, bf16[512,512]{1,0:T(8,128)(2,1)} %get-tuple-element.12.exg_ref, ...), custom_call_target="tpu_custom_call" | custom-call | tf_op jit(solution)/shard_map/mix_and_feed/pallas_call | solution.py:391
